TPU v7x, 32 devices: a whole 2x2x4 slice. The times are simulated.
32 devices in a mesh: row: 4 (over z), col: 4 (over x, core), depth: 2 (over y).
Axes of the slice: x: 2, y: 2, z: 4, core: 2. Of those that a mesh axis runs over, the one named last changes fastest.
Arguments:
- heads_concat: bfloat16 [2048, 16384], P('row', ('depth', 'col')), may hold values from -6 to 6
- w_out: bfloat16 [16384, 7168], P(('depth', 'row'), 'col'), may hold values from -0.046875 to 0.046875
Outputs:
- projected: bfloat16 [2048, 7168], P('row', ('col', 'depth'))
All inputs are finite; a program needn't handle non-finite values.
Results may differ from a plain program's by a relative error of at most 0.001.
Values may be sent and summed in bfloat16 or wider, within the bound.
A program may use at most 128 MiB of HBM per device.

v0:
```python
import functools

import jax
import jax.numpy as jnp
from jax import lax
from jax.experimental import pallas as pl
from jax.experimental.pallas import tpu as pltpu
from jax.sharding import PartitionSpec as P

MESH = pl.DeviceIdType.MESH
CORES = 2
LAG = 2
VMEM_BYTES = 66_000_000


def finishing(rows, r):
    downward = [(2 * t + rows - 1 - r, t) for t in range(r)]
    upward = [(2 * (rows - 1 - t) + r, t) for t in range(r + 1, rows)]
    return [t for _, t in sorted(downward + upward)] + [r]


def kernel(rows, cols, aligned, a_ref, w_ref, o_ref, w, a, own, out_y, in_y, chain,
           w_sem, s1_send, s1_recv, x_send, x_recv, c_send, c_recv, f_send, f_recv,
           y_send, y_recv, z_send, z_recv):
    r, j, d = lax.axis_index("row"), lax.axis_index("col"), lax.axis_index("depth")
    chips = cols // CORES
    x, core = j // CORES, j % CORES
    share = rows // cols
    tq, kb = a.shape[2], a.shape[3]
    nh = own.shape[3]
    steps = rows * cols
    mate = {"row": r, "col": x * CORES + 1 - core, "depth": d}
    across = {"row": r, "col": j, "depth": 1 - d}
    below = {"row": lax.rem(r + rows - 1, rows), "col": j, "depth": d}
    above = {"row": lax.rem(r + 1, rows), "col": j, "depth": d}
    source_col = r // share

    def x_col(dx):
        return lax.rem(x + dx, chips) * CORES + core

    def x_peer(dx):
        return {"row": r, "col": x_col(dx), "depth": d}

    w_copy = pltpu.make_async_copy(w_ref, w, w_sem)
    w_copy.start()

    barrier = pltpu.get_barrier_semaphore()

    def greet(device):
        pl.semaphore_signal(barrier, inc=1, device_id=device, device_id_type=MESH)

    for t in range(rows):
        pl.when(jnp.logical_or(r != t, source_col != j))(
            lambda t=t: greet({"row": t, "col": source_col, "depth": d})
        )
    for dx in range(1, chips):
        greet(x_peer(dx))
    greet(mate)
    greet(across)
    pl.when(r > 0)(lambda: greet(below))
    pl.when(r < rows - 1)(lambda: greet(above))
    pl.semaphore_wait(
        barrier,
        share * cols + chips
        + jnp.where(source_col != j, 1, 0)
        + jnp.where(r > 0, 1, 0)
        + jnp.where(r < rows - 1, 1, 0),
    )

    def remote(src, dst, send, recv, device):
        return pltpu.make_async_remote_copy(
            src_ref=src, dst_ref=dst, send_sem=send, recv_sem=recv,
            device_id=device, device_id_type=MESH,
        )

    def first(i, q):
        target = {"row": j * share + i, "col": q, "depth": d}
        source = a_ref.at[pl.ds(q * tq, tq), pl.ds(i * kb, kb)]
        return remote(source, a.at[r, q], s1_send.at[i, q], s1_recv.at[r], target)

    def is_me(i, q):
        return jnp.logical_and(r == j * share + i, j == q)

    for i in range(share):
        for q in range(cols):
            @pl.when(is_me(i, q))
            def _():
                pltpu.make_async_copy(
                    a_ref.at[pl.ds(q * tq, tq), pl.ds(i * kb, kb)],
                    a.at[r, q], s1_recv.at[r],
                ).start()

            @pl.when(jnp.logical_not(is_me(i, q)))
            def _():
                first(i, q).start()

    def to_x(t, dx):
        return remote(a.at[t, j], a.at[t, j], x_send.at[dx - 1, t], x_recv.at[dx - 1, t], x_peer(dx))

    def to_mate(t):
        return remote(a.at[t, j], a.at[t, j], c_send.at[t], c_recv.at[t], mate)

    def forward(t, dx):
        col = x_col(chips - dx)
        return remote(a.at[t, col], a.at[t, col], f_send.at[dx - 1, t], f_recv.at[dx - 1, t], mate)

    def arrived(slot, sem):
        pltpu.make_async_copy(slot, slot, sem).wait()

    def spread(t):
        arrived(a.at[t, j], s1_recv.at[t])
        for dx in range(1, chips):
            to_x(t, dx).start()
        to_mate(t).start()

    def relay(t):
        for dx in range(1, chips):
            arrived(a.at[t, x_col(chips - dx)], x_recv.at[dx - 1, t])
            forward(t, dx).start()

    def half(h):
        if aligned:
            return w[:, pl.ds(pl.multiple_of(h * nh, 128), nh)]
        return w[h]

    def y_copy(t, q):
        return remote(out_y.at[t, q], in_y.at[t, q], y_send.at[t, q], y_recv.at[t, q], across)

    def down(t, q):
        return remote(own.at[t, q], chain.at[t, q], z_send.at[t, q], z_recv.at[t, q], below)

    def up(t, q):
        return remote(own.at[t, q], chain.at[t + 1, q], z_send.at[t, q], z_recv.at[t + 1, q], above)

    order = []
    for p in range(rows):
        block = jnp.int32(0)
        for row in range(rows):
            block = jnp.where(r == row, finishing(rows, row)[p], block)
        order.append(block)

    def pick(p):
        block = order[0]
        for n in range(1, rows):
            block = jnp.where(p == n, order[n], block)
        return block

    def place(n):
        k = n // (CORES * (rows - 1)) * CORES + n % CORES
        return n // CORES % (rows - 1), k

    def column(k):
        chip = lax.rem(x + chips - k // CORES, chips)
        return chip * CORES + jnp.where(k % CORES == 0, core, 1 - core)

    def multiply(t, q):
        block = a[t, q]
        out_y[t, q] = jnp.dot(block, half(1 - d), preferred_element_type=jnp.float32)
        own[t, q] = jnp.dot(block, half(d), preferred_element_type=jnp.float32)
        y_copy(t, q).start()

    def finish(s):
        p, k = place(s)
        mine = s >= steps - cols
        t = jnp.where(mine, r, pick(p))
        q = column(jnp.where(mine, s - (steps - cols), k))
        arrived(in_y.at[t, q], y_recv.at[t, q])
        own[t, q] += in_y[t, q]

        @pl.when(jnp.logical_and(t <= r, r < rows - 1))
        def _():
            arrived(chain.at[t, q], z_recv.at[t, q])
            own[t, q] += chain[t, q]

        @pl.when(jnp.logical_and(t >= r, r > 0))
        def _():
            arrived(chain.at[t + 1, q], z_recv.at[t + 1, q])
            own[t, q] += chain[t + 1, q]

        pl.when(t < r)(lambda: down(t, q).start())
        pl.when(t > r)(lambda: up(t, q).start())

        @pl.when(t == r)
        def _():
            o_ref[pl.ds(pl.multiple_of(q * tq, tq), tq), :] = own[t, q].astype(o_ref.dtype)

    w_copy.wait()

    def step(s, carry):
        p, k = place(s - cols)
        mine = s < cols
        t = jnp.where(mine, r, pick(p))
        k = jnp.where(mine, s, k)

        pl.when(k == 0)(lambda: spread(t))

        @pl.when(k == 1)
        def _():
            arrived(a.at[t, column(1)], c_recv.at[t])

        pl.when(k == CORES)(lambda: relay(t))
        for dx in range(1, chips):
            @pl.when(k == CORES * dx + 1)
            def _():
                arrived(a.at[t, column(CORES * dx + 1)], f_recv.at[dx - 1, t])

        multiply(t, column(k))

        pl.when(s >= cols + LAG)(lambda: finish(s - cols - LAG))
        return carry

    lax.fori_loop(0, steps, step, 0)

    def last(s, carry):
        finish(s)
        return carry

    lax.fori_loop(steps - cols - LAG, steps, last, 0)

    for i in range(share):
        for q in range(cols):
            pl.when(jnp.logical_not(is_me(i, q)))(lambda i=i, q=q: first(i, q).wait_send())

    def drain(t, carry):
        for dx in range(1, chips):
            to_x(t, dx).wait_send()
            forward(t, dx).wait_send()
        to_mate(t).wait_send()
        for q in range(cols):
            y_copy(t, q).wait_send()
            pl.when(t != r)(lambda q=q: down(t, q).wait_send())
        return carry

    lax.fori_loop(0, rows, drain, 0)


def project(rows, cols, heads, w_out):
    tokens = heads.shape[0]
    kb, n = w_out.shape
    nh, tq = n // 2, tokens // cols
    chips = cols // CORES
    aligned = nh % 128 == 0
    w_shape = (kb, n)
    if not aligned:
        w_out = jnp.stack([w_out[:, :nh], w_out[:, nh:]])
        w_shape = (2, kb, nh)
    dma = pltpu.SemaphoreType.DMA
    f32 = jnp.float32
    return pl.pallas_call(
        functools.partial(kernel, rows, cols, aligned),
        out_shape=jax.ShapeDtypeStruct((tokens, nh), jnp.bfloat16),
        in_specs=[pl.BlockSpec(memory_space=pltpu.HBM)] * 2,
        out_specs=pl.BlockSpec(memory_space=pltpu.VMEM),
        scratch_shapes=[
            pltpu.VMEM(w_shape, jnp.bfloat16),
            pltpu.VMEM((rows, cols, tq, kb), jnp.bfloat16),
            pltpu.VMEM((rows, cols, tq, nh), f32),
            pltpu.VMEM((rows, cols, tq, nh), f32),
            pltpu.VMEM((rows, cols, tq, nh), f32),
            pltpu.VMEM((rows + 1, cols, tq, nh), f32),
            dma,
            dma((rows // cols, cols)), dma((rows,)),
            dma((chips - 1, rows)), dma((chips - 1, rows)),
            dma((rows,)), dma((rows,)),
            dma((chips - 1, rows)), dma((chips - 1, rows)),
            dma((rows, cols)), dma((rows, cols)),
            dma((rows, cols)), dma((rows + 1, cols)),
        ],
        compiler_params=pltpu.CompilerParams(
            collective_id=0, has_side_effects=True, vmem_limit_bytes=VMEM_BYTES
        ),
    )(heads, w_out)


def solution(mesh):
    rows, cols = mesh.shape["row"], mesh.shape["col"]

    def per_device(heads, w_out):
        tokens, n = heads.shape[0], w_out.shape[1]
        lanes = -(-n // 256) * 128
        slots = 17 * rows * tokens * lanes
        calls = 1
        while slots // calls > VMEM_BYTES // 2:
            calls *= 2
        size = tokens // calls
        parts = [
            project(rows, cols, heads[c * size:(c + 1) * size], w_out)
            for c in range(calls)
        ]
        return parts[0] if calls == 1 else jnp.concatenate(parts, axis=0)

    return jax.shard_map(
        per_device,
        mesh=mesh,
        in_specs=(P("row", ("depth", "col")), P(("depth", "row"), "col")),
        out_specs=P("row", ("col", "depth")),
        check_vma=False,
    )
```

profile of v0, /device:TPU:10, one launch (start us, length us, event | category | flops | bytes accessed | tf_op | source)
XLA Modules:
  0.0 212.0 jit_solution(12640694512669598213)
XLA Ops:
  0.0 209.8 %shard_map.28 = bf16[512,896]{1,0:T(8,128)(2,1)} custom-call(bf16[512,2048]{1,0:T(8,128)(2,1)} %a_ref.1, bf16[2048,1792]{1,0:T(8,128)(2,1)} %w_ref.1), custom_call_target="tpu_custom_call" | custom-call | tf_op jit(solution)/shard_map/pallas_call | solution.py:249
  209.8 2.2 %copy.4 = bf16[512,896]{1,0:T(8,128)(2,1)} copy(bf16[512,896]{1,0:T(8,128)(2,1)} %shard_map.28) | data formatting | bytes 1835008
where the time goes:
time: 216 us; the launch traced here: 212 us
  Pallas kernels  210 us (97%)
  local copies, waits for them, and re-layouts  2.18 us (1%)
    pallas_call x1, Pallas kernels, project(): pl.pallas_call(functools.partial(kernel, rows, cols, aligned), out_shape=...  210 us

commit v1 on v0

--- a/solution.py
+++ b/solution.py
@@ -11,6 +11,29 @@
 CORES = 2
 LAG = 2
 VMEM_BYTES = 66_000_000
+SQUARINGS = 5
+POWER = 2 ** SQUARINGS
+REACH = 125
+LOW = 2.0 ** (-REACH / POWER)
+SPAN = 2.0 ** (REACH / POWER) - LOW
+SMALLEST = 1e-36
+
+
+def encode(value, coded, scale):
+    largest = jnp.max(jnp.max(jnp.abs(value), axis=0, keepdims=True), axis=1, keepdims=True)
+    largest = jnp.maximum(largest, SMALLEST)
+    scale[...] = jnp.broadcast_to(largest, scale.shape)
+    power = LOW + jnp.abs(value) * (SPAN / largest)
+    for _ in range(SQUARINGS):
+        power = power * power
+    coded[...] = jnp.where(value < 0, -power, power).astype(coded.dtype)
+
+
+def decode(coded, scale):
+    power = coded[...].astype(jnp.float32)
+    root = jnp.exp2(jnp.log2(jnp.abs(power)) * (1.0 / POWER))
+    value = (root - LOW) * (scale[:, :1] * (1.0 / SPAN))
+    return jnp.where(power < 0, -value, value)
 
 
 def finishing(rows, r):
@@ -19,9 +42,10 @@
     return [t for _, t in sorted(downward + upward)] + [r]
 
 
-def kernel(rows, cols, aligned, a_ref, w_ref, o_ref, w, a, own, out_y, in_y, chain,
+def kernel(rows, cols, aligned, a_ref, w_ref, o_ref, w, a, own, out_y, in_y, out_z, chain,
+           out_ys, in_ys, out_zs, chain_s,
            w_sem, s1_send, s1_recv, x_send, x_recv, c_send, c_recv, f_send, f_recv,
-           y_send, y_recv, z_send, z_recv):
+           y_send, y_recv, z_send, z_recv, ys_send, ys_recv, zs_send, zs_recv):
     r, j, d = lax.axis_index("row"), lax.axis_index("col"), lax.axis_index("depth")
     chips = cols // CORES
     x, core = j // CORES, j % CORES
@@ -123,14 +147,31 @@
             return w[:, pl.ds(pl.multiple_of(h * nh, 128), nh)]
         return w[h]
 
-    def y_copy(t, q):
-        return remote(out_y.at[t, q], in_y.at[t, q], y_send.at[t, q], y_recv.at[t, q], across)
+    def y_copies(t, q):
+        return (
+            remote(out_y.at[t, q], in_y.at[t, q], y_send.at[t, q], y_recv.at[t, q], across),
+            remote(out_ys.at[t, q], in_ys.at[t, q], ys_send.at[t, q], ys_recv.at[t, q], across),
+        )
+
+    def z_copies(t, q, slot, device):
+        return (
+            remote(out_z.at[t, q], chain.at[slot, q], z_send.at[t, q], z_recv.at[slot, q], device),
+            remote(out_zs.at[t, q], chain_s.at[slot, q], zs_send.at[t, q], zs_recv.at[slot, q], device),
+        )
 
     def down(t, q):
-        return remote(own.at[t, q], chain.at[t, q], z_send.at[t, q], z_recv.at[t, q], below)
+        return z_copies(t, q, t, below)
 
     def up(t, q):
-        return remote(own.at[t, q], chain.at[t + 1, q], z_send.at[t, q], z_recv.at[t + 1, q], above)
+        return z_copies(t, q, t + 1, above)
+
+    def start(copies):
+        for copy in copies:
+            copy.start()
+
+    def wait_send(copies):
+        for copy in copies:
+            copy.wait_send()
 
     order = []
     for p in range(rows):
@@ -155,9 +196,10 @@
 
     def multiply(t, q):
         block = a[t, q]
-        out_y[t, q] = jnp.dot(block, half(1 - d), preferred_element_type=jnp.float32)
+        sent = jnp.dot(block, half(1 - d), preferred_element_type=jnp.float32)
+        encode(sent, out_y.at[t, q], out_ys.at[t, q])
+        start(y_copies(t, q))
         own[t, q] = jnp.dot(block, half(d), preferred_element_type=jnp.float32)
-        y_copy(t, q).start()
 
     def finish(s):
         p, k = place(s)
@@ -165,20 +207,19 @@
         t = jnp.where(mine, r, pick(p))
         q = column(jnp.where(mine, s - (steps - cols), k))
         arrived(in_y.at[t, q], y_recv.at[t, q])
-        own[t, q] += in_y[t, q]
-
-        @pl.when(jnp.logical_and(t <= r, r < rows - 1))
-        def _():
-            arrived(chain.at[t, q], z_recv.at[t, q])
-            own[t, q] += chain[t, q]
-
-        @pl.when(jnp.logical_and(t >= r, r > 0))
-        def _():
-            arrived(chain.at[t + 1, q], z_recv.at[t + 1, q])
-            own[t, q] += chain[t + 1, q]
-
-        pl.when(t < r)(lambda: down(t, q).start())
-        pl.when(t > r)(lambda: up(t, q).start())
+        arrived(in_ys.at[t, q], ys_recv.at[t, q])
+        own[t, q] += decode(in_y.at[t, q], in_ys.at[t, q])
+
+        def add(slot):
+            arrived(chain.at[slot, q], z_recv.at[slot, q])
+            arrived(chain_s.at[slot, q], zs_recv.at[slot, q])
+            own[t, q] += decode(chain.at[slot, q], chain_s.at[slot, q])
+
+        pl.when(jnp.logical_and(t <= r, r < rows - 1))(lambda: add(t))
+        pl.when(jnp.logical_and(t >= r, r > 0))(lambda: add(t + 1))
+        pl.when(t != r)(lambda: encode(own[t, q], out_z.at[t, q], out_zs.at[t, q]))
+        pl.when(t < r)(lambda: start(down(t, q)))
+        pl.when(t > r)(lambda: start(up(t, q)))
 
         @pl.when(t == r)
         def _():
@@ -227,8 +268,8 @@
             forward(t, dx).wait_send()
         to_mate(t).wait_send()
         for q in range(cols):
-            y_copy(t, q).wait_send()
-            pl.when(t != r)(lambda q=q: down(t, q).wait_send())
+            wait_send(y_copies(t, q))
+            pl.when(t != r)(lambda q=q: wait_send(down(t, q)))
         return carry
 
     lax.fori_loop(0, rows, drain, 0)
@@ -255,14 +296,21 @@
             pltpu.VMEM(w_shape, jnp.bfloat16),
             pltpu.VMEM((rows, cols, tq, kb), jnp.bfloat16),
             pltpu.VMEM((rows, cols, tq, nh), f32),
-            pltpu.VMEM((rows, cols, tq, nh), f32),
-            pltpu.VMEM((rows, cols, tq, nh), f32),
-            pltpu.VMEM((rows + 1, cols, tq, nh), f32),
+            pltpu.VMEM((rows, cols, tq, nh), jnp.bfloat16),
+            pltpu.VMEM((rows, cols, tq, nh), jnp.bfloat16),
+            pltpu.VMEM((rows, cols, tq, nh), jnp.bfloat16),
+            pltpu.VMEM((rows + 1, cols, tq, nh), jnp.bfloat16),
+            pltpu.VMEM((rows, cols, 1, 128), f32),
+            pltpu.VMEM((rows, cols, 1, 128), f32),
+            pltpu.VMEM((rows, cols, 1, 128), f32),
+            pltpu.VMEM((rows + 1, cols, 1, 128), f32),
             dma,
             dma((rows // cols, cols)), dma((rows,)),
             dma((chips - 1, rows)), dma((chips - 1, rows)),
             dma((rows,)), dma((rows,)),
             dma((chips - 1, rows)), dma((chips - 1, rows)),
+            dma((rows, cols)), dma((rows, cols)),
+            dma((rows, cols)), dma((rows + 1, cols)),
             dma((rows, cols)), dma((rows, cols)),
             dma((rows, cols)), dma((rows + 1, cols)),
         ],

time: 216 us -> 164 us (0.76); the launches traced: 212 us -> 164 us
  Pallas kernels: 210 us -> 161 us
    pallas_call x1, Pallas kernels: 210 us -> 161 us  [project(): pl.pallas_call(functools.partial(kernel, rows, cols, aligned), out_shape=...]
where the time goes in v1:
time: 164 us
  Pallas kernels  161 us (98%)
  local copies, waits for them, and re-layouts  2.18 us (1%)
    pallas_call x1, Pallas kernels, project(): pl.pallas_call(functools.partial(kernel, rows, cols, aligned), out_shape=...  161 us

profile of v1, /device:TPU:10, one launch (start us, length us, event | category | flops | bytes accessed | tf_op | source)
XLA Modules:
  0.0 163.6 jit_solution(17652422949275080360)
XLA Ops:
  0.0 161.4 %shard_map.28 = bf16[512,896]{1,0:T(8,128)(2,1)} custom-call(bf16[512,2048]{1,0:T(8,128)(2,1)} %a_ref.1, bf16[2048,1792]{1,0:T(8,128)(2,1)} %w_ref.1), custom_call_target="tpu_custom_call" | custom-call | tf_op jit(solution)/shard_map/pallas_call | solution.py:290
  161.4 2.2 %copy.4 = bf16[512,896]{1,0:T(8,128)(2,1)} copy(bf16[512,896]{1,0:T(8,128)(2,1)} %shard_map.28) | data formatting | bytes 1835008

commit v2 on v1

--- a/solution.py
+++ b/solution.py
@@ -9,7 +9,16 @@
 
 MESH = pl.DeviceIdType.MESH
 CORES = 2
-LAG = 2
+LAGS = (6, 1, 2)
+CALM_STEP = (2, 0)
+PASS_STEPS = ((0, 0), (1, 0))
+FEED_STEP = 1
+PASS_CALM = (1, 1)
+SPREAD_NEAR = (1, -1)
+SPREAD_FAR = (0, 0)
+RELAY_NEAR = (4, 6)
+RELAY_FAR = (2, 2)
+ADJOINING_X = (5, 7)
 VMEM_BYTES = 66_000_000
 SQUARINGS = 5
 POWER = 2 ** SQUARINGS
@@ -36,15 +45,39 @@
     return jnp.where(power < 0, -value, value)
 
 
-def finishing(rows, r):
+def adjoining(row):
+    return row + 1 - 2 * (row % 2)
+
+
+def finishing(rows, r, near, paired):
     downward = [(2 * t + rows - 1 - r, t) for t in range(r)]
     upward = [(2 * (rows - 1 - t) + r, t) for t in range(r + 1, rows)]
-    return [t for _, t in sorted(downward + upward)] + [r]
-
-
-def kernel(rows, cols, aligned, a_ref, w_ref, o_ref, w, a, own, out_y, in_y, out_z, chain,
+    everyone = [t for _, t in sorted(downward + upward)]
+    if not paired:
+        return everyone
+    others = [t for t in everyone if t != adjoining(r)]
+    return [adjoining(r)] + others if near else others + [adjoining(r)]
+
+
+def pairable(rows, cols):
+    for x in range(cols // CORES):
+        place = {}
+        for r in range(rows):
+            near = r * cols // rows // CORES == x
+            for p, t in enumerate(finishing(rows, r, near, True)):
+                place[r, t] = p
+        for r, t in place:
+            before = (r + 1, t) if t < r else (r - 1, t)
+            if place.get(before, 0) > place[r, t]:
+                return False
+    return True
+
+
+def kernel(rows, cols, aligned, a_ref, w_ref, o_ref, w, a, via, own, out_y, in_y, out_z, chain,
            out_ys, in_ys, out_zs, chain_s,
-           w_sem, s1_send, s1_recv, x_send, x_recv, c_send, c_recv, f_send, f_recv,
+           w_sem, own_x_send, own_m_send, own_recv, adj_send, adj_x_send, adj_recv, adj_m_send, adj_m_recv,
+           v_send, v_recv, s1_send, s1_recv,
+           x_send, x_recv, c_send, c_recv, f_send, f_recv,
            y_send, y_recv, z_send, z_recv, ys_send, ys_recv, zs_send, zs_recv):
     r, j, d = lax.axis_index("row"), lax.axis_index("col"), lax.axis_index("depth")
     chips = cols // CORES
@@ -58,9 +91,18 @@
     below = {"row": lax.rem(r + rows - 1, rows), "col": j, "depth": d}
     above = {"row": lax.rem(r + 1, rows), "col": j, "depth": d}
     source_col = r // share
+    source_x, source_core = source_col // CORES, source_col % CORES
+    home = j == source_col
+    paired = pairable(rows, cols)
+    near = jnp.logical_and(x == source_x, paired)
+    edge = jnp.logical_or(r == 0, r == rows - 1)
+    beside = adjoining(r) if paired else -1
+
+    def x_at(dx):
+        return lax.rem(x + dx, chips)
 
     def x_col(dx):
-        return lax.rem(x + dx, chips) * CORES + core
+        return x_at(dx) * CORES + core
 
     def x_peer(dx):
         return {"row": r, "col": x_col(dx), "depth": d}
@@ -74,8 +116,8 @@
         pl.semaphore_signal(barrier, inc=1, device_id=device, device_id_type=MESH)
 
     for t in range(rows):
-        pl.when(jnp.logical_or(r != t, source_col != j))(
-            lambda t=t: greet({"row": t, "col": source_col, "depth": d})
+        pl.when(r != t)(
+            lambda t=t: greet({"row": t, "col": x * CORES + source_core, "depth": d})
         )
     for dx in range(1, chips):
         greet(x_peer(dx))
@@ -85,8 +127,7 @@
     pl.when(r < rows - 1)(lambda: greet(above))
     pl.semaphore_wait(
         barrier,
-        share * cols + chips
-        + jnp.where(source_col != j, 1, 0)
+        CORES * (rows // CORES - jnp.where(source_core == core, 1, 0)) + chips + 1
         + jnp.where(r > 0, 1, 0)
         + jnp.where(r < rows - 1, 1, 0),
     )
@@ -97,26 +138,117 @@
             device_id=device, device_id_type=MESH,
         )
 
-    def first(i, q):
-        target = {"row": j * share + i, "col": q, "depth": d}
-        source = a_ref.at[pl.ds(q * tq, tq), pl.ds(i * kb, kb)]
-        return remote(source, a.at[r, q], s1_send.at[i, q], s1_recv.at[r], target)
-
-    def is_me(i, q):
-        return jnp.logical_and(r == j * share + i, j == q)
+    def arrived(slot, sem):
+        pltpu.make_async_copy(slot, slot, sem).wait()
+
+    def piece(i, q):
+        return a_ref.at[pl.ds(pl.multiple_of(q * tq, tq), tq), pl.ds(pl.multiple_of(i * kb, kb), kb)]
+
+    def target(dx, i):
+        return x_col(chips - dx) * share + i
+
+    def away(dx, i):
+        return jnp.logical_and(target(dx, i) != r, target(dx, i) != beside)
+
+    def urgent(dx, i):
+        return r == jnp.where(target(dx, i) < rows // 2, rows - 1, 0)
+
+    def send(dx, i, c):
+        col = x * CORES + c
+        source = via.at[dx - 1, i, c] if dx else piece(i, col)
+        device = {"row": target(dx, i), "col": col, "depth": d}
+        return remote(source, a.at[r, col], s1_send.at[dx, i, c], s1_recv.at[r], device)
+
+    def aside(dx, i, c):
+        return remote(
+            piece(i, x_at(dx) * CORES + c), via.at[dx - 1, i, c],
+            v_send.at[dx - 1, i, c], v_recv.at[dx - 1, i, c], x_peer(dx),
+        )
+
+    def own_x(dx, q):
+        return remote(piece(r % share, q), a.at[r, q], own_x_send.at[dx - 1, q], own_recv.at[q], x_peer(dx))
+
+    def own_mate(q, source):
+        return remote(source, a.at[r, q], own_m_send.at[q], own_recv.at[q], mate)
+
+    def early(dx, i):
+        return jnp.logical_or(urgent(dx, i), x_at(chips - dx) != source_x)
+
+    def column(k):
+        chip = lax.rem(x + chips - k // CORES, chips)
+        return chip * CORES + jnp.where(k % CORES == 0, core, 1 - core)
+
+    def adjoin(e, c):
+        col = lax.rem(x + chips - e, chips) * CORES + c
+        device = {"row": beside, "col": x * CORES + c, "depth": d}
+        return remote(piece(beside % share, col), a.at[r, col], adj_send.at[e, c], adj_recv.at[e], device)
+
+    def adjoin_x(e, dx):
+        slot = a.at[beside, column(CORES * e)]
+        index = lax.rem(e + dx, chips)
+        return remote(slot, slot, adj_x_send.at[dx - 1, e], adj_recv.at[index], x_peer(dx))
+
+    def adjoin_mate(e):
+        slot = a.at[beside, column(CORES * e)]
+        return remote(slot, slot, adj_m_send.at[e], adj_m_recv.at[e], mate)
+
+    feeds = jnp.logical_and(beside // share == j, paired)
+
+    def feed(es):
+        @pl.when(feeds)
+        def _():
+            for e in es:
+                for c in range(CORES):
+                    adjoin(e, c).start()
+
+    feed([0])
 
     for i in range(share):
+        for c in range(CORES):
+            pl.when(jnp.logical_and(away(0, i), urgent(0, i)))(lambda i=i, c=c: send(0, i, c).start())
+            for dx in range(1, chips):
+                pl.when(away(0, i))(lambda dx=dx, i=i, c=c: aside(dx, i, c).start())
+
+    @pl.when(home)
+    def _():
         for q in range(cols):
-            @pl.when(is_me(i, q))
-            def _():
-                pltpu.make_async_copy(
-                    a_ref.at[pl.ds(q * tq, tq), pl.ds(i * kb, kb)],
-                    a.at[r, q], s1_recv.at[r],
-                ).start()
-
-            @pl.when(jnp.logical_not(is_me(i, q)))
-            def _():
-                first(i, q).start()
+            pltpu.make_async_copy(piece(r % share, q), a.at[r, q], own_recv.at[q]).start()
+            own_mate(q, piece(r % share, q)).start()
+            for dx in range(1, chips):
+                own_x(dx, q).start()
+
+    carrier = jnp.logical_and(core == source_core, x != source_x)
+
+    def own_ready(q):
+        arrived(a.at[r, q], own_recv.at[q])
+        pl.when(carrier)(lambda: own_mate(q, a.at[r, q]).start())
+
+    def calm(dx, i):
+        return jnp.logical_not(urgent(dx, i))
+
+    def each(dxs, cs, chosen, act):
+        for i in range(share):
+            for c in cs:
+                for dx in dxs:
+                    pl.when(jnp.logical_and(away(dx, i), chosen(dx, i)))(
+                        lambda dx=dx, i=i, c=c: act(dx, i, c)
+                    )
+
+    def pass_on(dx, i, c):
+        arrived(via.at[dx - 1, i, c], v_recv.at[dx - 1, i, c])
+        send(dx, i, c).start()
+
+    def adjoining_ready(k):
+        e = k // CORES
+
+        @pl.when(k % CORES == 0)
+        def _():
+            arrived(a.at[beside, column(k)], adj_recv.at[e])
+            adjoin_mate(e).start()
+
+        @pl.when(k % CORES == 1)
+        def _():
+            arrived(a.at[beside, column(k)], adj_m_recv.at[e])
 
     def to_x(t, dx):
         return remote(a.at[t, j], a.at[t, j], x_send.at[dx - 1, t], x_recv.at[dx - 1, t], x_peer(dx))
@@ -127,9 +259,6 @@
     def forward(t, dx):
         col = x_col(chips - dx)
         return remote(a.at[t, col], a.at[t, col], f_send.at[dx - 1, t], f_recv.at[dx - 1, t], mate)
-
-    def arrived(slot, sem):
-        pltpu.make_async_copy(slot, slot, sem).wait()
 
     def spread(t):
         arrived(a.at[t, j], s1_recv.at[t])
@@ -174,25 +303,31 @@
             copy.wait_send()
 
     order = []
-    for p in range(rows):
+    for p in range(rows - 1):
         block = jnp.int32(0)
         for row in range(rows):
-            block = jnp.where(r == row, finishing(rows, row)[p], block)
+            close, distant = finishing(rows, row, True, paired)[p], finishing(rows, row, False, paired)[p]
+            block = jnp.where(r == row, jnp.where(near, close, distant), block)
         order.append(block)
 
     def pick(p):
         block = order[0]
-        for n in range(1, rows):
+        for n in range(1, rows - 1):
             block = jnp.where(p == n, order[n], block)
         return block
 
-    def place(n):
-        k = n // (CORES * (rows - 1)) * CORES + n % CORES
-        return n // CORES % (rows - 1), k
-
-    def column(k):
-        chip = lax.rem(x + chips - k // CORES, chips)
-        return chip * CORES + jnp.where(k % CORES == 0, core, 1 - core)
+    def tile(n):
+        block, k = n // cols, n % cols
+        if not paired:
+            return pick(block), k
+        first = n < CORES
+        inner = jnp.logical_and(n >= CORES, n < CORES + cols)
+        outer = jnp.logical_and(n >= CORES + cols, n < 2 * cols)
+        near_t = jnp.where(inner, pick(1), jnp.where(jnp.logical_or(first, outer), beside, pick(block)))
+        near_k = jnp.where(inner, n - CORES, jnp.where(outer, n - cols, k))
+        far_t = pick(block)
+        far_k = jnp.where(far_t == beside, (k + CORES) % cols, k)
+        return jnp.where(near, near_t, far_t), jnp.where(near, near_k, far_k)
 
     def multiply(t, q):
         block = a[t, q]
@@ -202,10 +337,10 @@
         own[t, q] = jnp.dot(block, half(d), preferred_element_type=jnp.float32)
 
     def finish(s):
-        p, k = place(s)
         mine = s >= steps - cols
-        t = jnp.where(mine, r, pick(p))
-        q = column(jnp.where(mine, s - (steps - cols), k))
+        t, k = tile(jnp.where(mine, 0, s))
+        t = jnp.where(mine, r, t)
+        q = jnp.where(mine, s % cols, column(k))
         arrived(in_y.at[t, q], y_recv.at[t, q])
         arrived(in_ys.at[t, q], ys_recv.at[t, q])
         own[t, q] += decode(in_y.at[t, q], in_ys.at[t, q])
@@ -227,27 +362,67 @@
 
     w_copy.wait()
 
+    lag = jnp.where(near, jnp.where(edge, LAGS[2], LAGS[0]), LAGS[1])
+
+    def at(s, near_step, far_step):
+        return s == jnp.where(near, near_step, far_step)
+
+    def split(p):
+        return jnp.where(near, pick(min(p + 1, rows - 2)), pick(p))
+
     def step(s, carry):
-        p, k = place(s - cols)
         mine = s < cols
-        t = jnp.where(mine, r, pick(p))
+        t, k = tile(jnp.where(mine, 0, s - cols))
+        t = jnp.where(mine, r, t)
         k = jnp.where(mine, s, k)
-
-        pl.when(k == 0)(lambda: spread(t))
-
-        @pl.when(k == 1)
+        q = jnp.where(mine, k, column(k))
+        adjoined = jnp.logical_and(jnp.logical_not(mine), t == beside)
+        divided = jnp.logical_and(jnp.logical_not(mine), t != beside)
+        peers = range(1, chips)
+
+        for c in range(CORES):
+            pl.when(at(s, cols + PASS_STEPS[c][0], cols + PASS_STEPS[c][1]))(
+                lambda c=c: each(peers, [c], urgent, pass_on)
+            )
+        pl.when(at(s, cols + FEED_STEP, cols))(lambda: feed(range(1, chips)))
+        pl.when(at(s, cols + CALM_STEP[0], cols + CALM_STEP[1]))(
+            lambda: each([0], range(CORES), calm, lambda dx, i, c: send(dx, i, c).start())
+        )
+        pl.when(at(s, cols + PASS_CALM[0], cols + PASS_CALM[1]))(
+            lambda: each(peers, range(CORES), calm, pass_on)
+        )
+        for p in range(rows - 2 if paired else rows - 1):
+            base = cols * (p + 1)
+
+            @pl.when(at(s, base + SPREAD_NEAR[min(p, 1)], base + SPREAD_FAR[min(p, 1)]))
+            def _():
+                spread(split(p))
+
+            @pl.when(at(s, base + RELAY_NEAR[min(p, 1)], base + RELAY_FAR[min(p, 1)]))
+            def _():
+                relay(split(p))
+
+        for e in range(chips):
+            @pl.when(jnp.logical_and(near, s == cols + ADJOINING_X[min(e, 1)]))
+            def _():
+                for dx in peers:
+                    adjoin_x(e, dx).start()
+
+        pl.when(mine)(lambda: own_ready(k))
+        pl.when(adjoined)(lambda: adjoining_ready(k))
+
+        @pl.when(jnp.logical_and(divided, k == 1))
         def _():
             arrived(a.at[t, column(1)], c_recv.at[t])
 
-        pl.when(k == CORES)(lambda: relay(t))
-        for dx in range(1, chips):
-            @pl.when(k == CORES * dx + 1)
+        for dx in peers:
+            @pl.when(jnp.logical_and(divided, k == CORES * dx + 1))
             def _():
                 arrived(a.at[t, column(CORES * dx + 1)], f_recv.at[dx - 1, t])
 
-        multiply(t, column(k))
-
-        pl.when(s >= cols + LAG)(lambda: finish(s - cols - LAG))
+        multiply(t, q)
+
+        pl.when(s >= cols + lag)(lambda: finish(s - cols - lag))
         return carry
 
     lax.fori_loop(0, steps, step, 0)
@@ -256,17 +431,39 @@
         finish(s)
         return carry
 
-    lax.fori_loop(steps - cols - LAG, steps, last, 0)
+    lax.fori_loop(steps - cols - lag, steps, last, 0)
+
+    for e in range(chips):
+        for c in range(CORES):
+            pl.when(feeds)(lambda e=e, c=c: adjoin(e, c).wait_send())
+        pl.when(paired)(lambda e=e: adjoin_mate(e).wait_send())
+        for dx in range(1, chips):
+            pl.when(near)(lambda e=e, dx=dx: adjoin_x(e, dx).wait_send())
 
     for i in range(share):
-        for q in range(cols):
-            pl.when(jnp.logical_not(is_me(i, q)))(lambda i=i, q=q: first(i, q).wait_send())
+        for c in range(CORES):
+            for dx in range(chips):
+                pl.when(away(dx, i))(lambda dx=dx, i=i, c=c: send(dx, i, c).wait_send())
+                if dx:
+                    pl.when(away(0, i))(lambda dx=dx, i=i, c=c: aside(dx, i, c).wait_send())
+
+    for q in range(cols):
+        @pl.when(core == source_core)
+        def _():
+            own_mate(q, a.at[r, q]).wait_send()
+
+        @pl.when(home)
+        def _():
+            for dx in range(1, chips):
+                own_x(dx, q).wait_send()
 
     def drain(t, carry):
-        for dx in range(1, chips):
-            to_x(t, dx).wait_send()
-            forward(t, dx).wait_send()
-        to_mate(t).wait_send()
+        @pl.when(jnp.logical_and(t != r, t != beside))
+        def _():
+            for dx in range(1, chips):
+                to_x(t, dx).wait_send()
+                forward(t, dx).wait_send()
+            to_mate(t).wait_send()
         for q in range(cols):
             wait_send(y_copies(t, q))
             pl.when(t != r)(lambda q=q: wait_send(down(t, q)))
@@ -279,7 +476,7 @@
     tokens = heads.shape[0]
     kb, n = w_out.shape
     nh, tq = n // 2, tokens // cols
-    chips = cols // CORES
+    chips, share = cols // CORES, rows // cols
     aligned = nh % 128 == 0
     w_shape = (kb, n)
     if not aligned:
@@ -295,6 +492,7 @@
         scratch_shapes=[
             pltpu.VMEM(w_shape, jnp.bfloat16),
             pltpu.VMEM((rows, cols, tq, kb), jnp.bfloat16),
+            pltpu.VMEM((chips - 1, share, CORES, tq, kb), jnp.bfloat16),
             pltpu.VMEM((rows, cols, tq, nh), f32),
             pltpu.VMEM((rows, cols, tq, nh), jnp.bfloat16),
             pltpu.VMEM((rows, cols, tq, nh), jnp.bfloat16),
@@ -305,7 +503,10 @@
             pltpu.VMEM((rows, cols, 1, 128), f32),
             pltpu.VMEM((rows + 1, cols, 1, 128), f32),
             dma,
-            dma((rows // cols, cols)), dma((rows,)),
+            dma((chips - 1, cols)), dma((cols,)), dma((cols,)),
+            dma((chips, CORES)), dma((chips - 1, chips)), dma((chips,)), dma((chips,)), dma((chips,)),
+            dma((chips - 1, share, CORES)), dma((chips - 1, share, CORES)),
+            dma((chips, share, CORES)), dma((rows,)),
             dma((chips - 1, rows)), dma((chips - 1, rows)),
             dma((rows,)), dma((rows,)),
             dma((chips - 1, rows)), dma((chips - 1, rows)),

time: 164 us -> 125 us (0.76)
  Pallas kernels: 161 us -> 122 us
    pallas_call x1, Pallas kernels: 161 us -> 122 us  [project(): pl.pallas_call(functools.partial(kernel, rows, cols, aligned), out_shape=...]
where the time goes in v2:
time: 125 us
  Pallas kernels  122 us (98%)
  local copies, waits for them, and re-layouts  2.18 us (2%)
    pallas_call x1, Pallas kernels, project(): pl.pallas_call(functools.partial(kernel, rows, cols, aligned), out_shape=...  122 us

profile of v2, /device:TPU:10, one launch (start us, length us, event | category | flops | bytes accessed | tf_op | source)
XLA Modules:
  0.0 124.6 jit_solution(18020023783492474458)
XLA Ops:
  0.0 122.4 %shard_map.28 = bf16[512,896]{1,0:T(8,128)(2,1)} custom-call(bf16[512,2048]{1,0:T(8,128)(2,1)} %a_ref.1, bf16[2048,1792]{1,0:T(8,128)(2,1)} %w_ref.1), custom_call_target="tpu_custom_call" | custom-call | tf_op jit(solution)/shard_map/pallas_call | solution.py:487
  122.5 2.2 %copy.4 = bf16[512,896]{1,0:T(8,128)(2,1)} copy(bf16[512,896]{1,0:T(8,128)(2,1)} %shard_map.28) | data formatting | bytes 1835008

commit v3 on v2

--- a/solution.py
+++ b/solution.py
@@ -9,12 +9,13 @@
 
 MESH = pl.DeviceIdType.MESH
 CORES = 2
-LAGS = (6, 1, 2)
-CALM_STEP = (2, 0)
+LAGS = (5, 1, 1)
+GRAIN = 2
+CALM_STEP = (2, -3)
 PASS_STEPS = ((0, 0), (1, 0))
 FEED_STEP = 1
 PASS_CALM = (1, 1)
-SPREAD_NEAR = (1, -1)
+SPREAD_NEAR = (1, 0)
 SPREAD_FAR = (0, 0)
 RELAY_NEAR = (4, 6)
 RELAY_FAR = (2, 2)
@@ -141,9 +142,20 @@
     def arrived(slot, sem):
         pltpu.make_async_copy(slot, slot, sem).wait()
 
+    grain = s1_recv.shape[1]
+    ts = tq // grain
+
     def piece(i, q):
         return a_ref.at[pl.ds(pl.multiple_of(q * tq, tq), tq), pl.ds(pl.multiple_of(i * kb, kb), kb)]
 
+    def part(i, q, g):
+        return a_ref.at[
+            pl.ds(pl.multiple_of(q * tq + g * ts, ts), ts), pl.ds(pl.multiple_of(i * kb, kb), kb)
+        ]
+
+    def sub(g):
+        return pl.ds(g * ts, ts)
+
     def target(dx, i):
         return x_col(chips - dx) * share + i
 
@@ -153,17 +165,25 @@
     def urgent(dx, i):
         return r == jnp.where(target(dx, i) < rows // 2, rows - 1, 0)
 
-    def send(dx, i, c):
+    def send(dx, i, c, g):
         col = x * CORES + c
-        source = via.at[dx - 1, i, c] if dx else piece(i, col)
+        source = via.at[dx - 1, i, c, sub(g)] if dx else part(i, col, g)
         device = {"row": target(dx, i), "col": col, "depth": d}
-        return remote(source, a.at[r, col], s1_send.at[dx, i, c], s1_recv.at[r], device)
-
-    def aside(dx, i, c):
+        return remote(source, a.at[r, col, sub(g)], s1_send.at[dx, i, c, g], s1_recv.at[r, g], device)
+
+    def aside(dx, i, c, g):
         return remote(
-            piece(i, x_at(dx) * CORES + c), via.at[dx - 1, i, c],
-            v_send.at[dx - 1, i, c], v_recv.at[dx - 1, i, c], x_peer(dx),
-        )
+            part(i, x_at(dx) * CORES + c, g), via.at[dx - 1, i, c, sub(g)],
+            v_send.at[dx - 1, i, c, g], v_recv.at[dx - 1, i, c, g], x_peer(dx),
+        )
+
+    def start_send(dx, i, c):
+        for g in range(grain):
+            send(dx, i, c, g).start()
+
+    def start_aside(dx, i, c):
+        for g in range(grain):
+            aside(dx, i, c, g).start()
 
     def own_x(dx, q):
         return remote(piece(r % share, q), a.at[r, q], own_x_send.at[dx - 1, q], own_recv.at[q], x_peer(dx))
@@ -205,9 +225,9 @@
 
     for i in range(share):
         for c in range(CORES):
-            pl.when(jnp.logical_and(away(0, i), urgent(0, i)))(lambda i=i, c=c: send(0, i, c).start())
+            pl.when(jnp.logical_and(away(0, i), urgent(0, i)))(lambda i=i, c=c: start_send(0, i, c))
             for dx in range(1, chips):
-                pl.when(away(0, i))(lambda dx=dx, i=i, c=c: aside(dx, i, c).start())
+                pl.when(away(0, i))(lambda dx=dx, i=i, c=c: start_aside(dx, i, c))
 
     @pl.when(home)
     def _():
@@ -235,8 +255,9 @@
                     )
 
     def pass_on(dx, i, c):
-        arrived(via.at[dx - 1, i, c], v_recv.at[dx - 1, i, c])
-        send(dx, i, c).start()
+        for g in range(grain):
+            arrived(via.at[dx - 1, i, c, sub(g)], v_recv.at[dx - 1, i, c, g])
+            send(dx, i, c, g).start()
 
     def adjoining_ready(k):
         e = k // CORES
@@ -250,8 +271,9 @@
         def _():
             arrived(a.at[beside, column(k)], adj_m_recv.at[e])
 
-    def to_x(t, dx):
-        return remote(a.at[t, j], a.at[t, j], x_send.at[dx - 1, t], x_recv.at[dx - 1, t], x_peer(dx))
+    def to_x(t, dx, g):
+        slot = a.at[t, j, sub(g)]
+        return remote(slot, slot, x_send.at[dx - 1, t, g], x_recv.at[dx - 1, t], x_peer(dx))
 
     def to_mate(t):
         return remote(a.at[t, j], a.at[t, j], c_send.at[t], c_recv.at[t], mate)
@@ -261,9 +283,10 @@
         return remote(a.at[t, col], a.at[t, col], f_send.at[dx - 1, t], f_recv.at[dx - 1, t], mate)
 
     def spread(t):
-        arrived(a.at[t, j], s1_recv.at[t])
-        for dx in range(1, chips):
-            to_x(t, dx).start()
+        for g in range(grain):
+            arrived(a.at[t, j, sub(g)], s1_recv.at[t, g])
+            for dx in range(1, chips):
+                to_x(t, dx, g).start()
         to_mate(t).start()
 
     def relay(t):
@@ -386,7 +409,7 @@
             )
         pl.when(at(s, cols + FEED_STEP, cols))(lambda: feed(range(1, chips)))
         pl.when(at(s, cols + CALM_STEP[0], cols + CALM_STEP[1]))(
-            lambda: each([0], range(CORES), calm, lambda dx, i, c: send(dx, i, c).start())
+            lambda: each([0], range(CORES), calm, start_send)
         )
         pl.when(at(s, cols + PASS_CALM[0], cols + PASS_CALM[1]))(
             lambda: each(peers, range(CORES), calm, pass_on)
@@ -443,9 +466,10 @@
     for i in range(share):
         for c in range(CORES):
             for dx in range(chips):
-                pl.when(away(dx, i))(lambda dx=dx, i=i, c=c: send(dx, i, c).wait_send())
-                if dx:
-                    pl.when(away(0, i))(lambda dx=dx, i=i, c=c: aside(dx, i, c).wait_send())
+                for g in range(grain):
+                    pl.when(away(dx, i))(lambda dx=dx, i=i, c=c, g=g: send(dx, i, c, g).wait_send())
+                    if dx:
+                        pl.when(away(0, i))(lambda dx=dx, i=i, c=c, g=g: aside(dx, i, c, g).wait_send())
 
     for q in range(cols):
         @pl.when(core == source_core)
@@ -461,7 +485,8 @@
         @pl.when(jnp.logical_and(t != r, t != beside))
         def _():
             for dx in range(1, chips):
-                to_x(t, dx).wait_send()
+                for g in range(grain):
+                    to_x(t, dx, g).wait_send()
                 forward(t, dx).wait_send()
             to_mate(t).wait_send()
         for q in range(cols):
@@ -477,6 +502,7 @@
     kb, n = w_out.shape
     nh, tq = n // 2, tokens // cols
     chips, share = cols // CORES, rows // cols
+    grain = GRAIN if tq % (16 * GRAIN) == 0 else 1
     aligned = nh % 128 == 0
     w_shape = (kb, n)
     if not aligned:
@@ -505,9 +531,9 @@
             dma,
             dma((chips - 1, cols)), dma((cols,)), dma((cols,)),
             dma((chips, CORES)), dma((chips - 1, chips)), dma((chips,)), dma((chips,)), dma((chips,)),
-            dma((chips - 1, share, CORES)), dma((chips - 1, share, CORES)),
-            dma((chips, share, CORES)), dma((rows,)),
-            dma((chips - 1, rows)), dma((chips - 1, rows)),
+            dma((chips - 1, share, CORES, grain)), dma((chips - 1, share, CORES, grain)),
+            dma((chips, share, CORES, grain)), dma((rows, grain)),
+            dma((chips - 1, rows, grain)), dma((chips - 1, rows)),
             dma((rows,)), dma((rows,)),
             dma((chips - 1, rows)), dma((chips - 1, rows)),
             dma((rows, cols)), dma((rows, cols)),

time: 125 us -> 123 us (0.984)
    pallas_call x1, Pallas kernels: 122 us -> 121 us  [project(): pl.pallas_call(functools.partial(kernel, rows, cols, aligned), out_shape=...]
where the time goes in v3:
time: 123 us
  Pallas kernels  121 us (98%)
  local copies, waits for them, and re-layouts  2.18 us (2%)
    pallas_call x1, Pallas kernels, project(): pl.pallas_call(functools.partial(kernel, rows, cols, aligned), out_shape=...  121 us

profile of v3, /device:TPU:10, one launch (start us, length us, event | category | flops | bytes accessed | tf_op | source)
XLA Modules:
  0.0 123.1 jit_solution(6986633825522636889)
XLA Ops:
  0.0 120.9 %shard_map.28 = bf16[512,896]{1,0:T(8,128)(2,1)} custom-call(bf16[512,2048]{1,0:T(8,128)(2,1)} %a_ref.1, bf16[2048,1792]{1,0:T(8,128)(2,1)} %w_ref.1), custom_call_target="tpu_custom_call" | custom-call | tf_op jit(solution)/shard_map/pallas_call | solution.py:513
  120.9 2.2 %copy.4 = bf16[512,896]{1,0:T(8,128)(2,1)} copy(bf16[512,896]{1,0:T(8,128)(2,1)} %shard_map.28) | data formatting | bytes 1835008
